TPU v7x, 32 devices: a whole 2x2x4 slice. The times are simulated.
32 devices in a mesh: section: 4 (over x, core), shard: 2 (over y), replica: 4 (over z).
Axes of the slice: x: 2, y: 2, z: 4, core: 2. Of those that a mesh axis runs over, the one named last changes fastest.
Arguments:
- acts_fwd: bfloat16 [4, 1024, 4096], P('section', ('shard', 'replica')), may hold values from -30 to 30
- pos_fwd: int32 [4, 1024], P('section', ('shard', 'replica')), may hold values from 0 to 2047
- saved_acts: bfloat16 [4, 1024, 4096], P('section', ('shard', 'replica')), may hold values from -30 to 30
- pos_bwd: int32 [4, 1024], P('section', ('shard', 'replica')), may hold values from 0 to 2047
- grads_in: bfloat16 [4, 1024, 4096], P('section', ('shard', 'replica')), may hold values from -6 to 6
- key_cotan: bfloat16 [4, 1024, 512], P('section', ('shard', 'replica')), may hold values from -6 to 6
- weight: bfloat16 [4, 4096, 512], P('section', 'shard'), may hold values from -0.09375 to 0.09375
- gain: float32 [4, 4096], P('section'), may hold values from 0.1 to 1.9
Outputs:
- keys: bfloat16 [4, 1024, 512], P('section', ('shard', 'replica'))
- grad_out: bfloat16 [4, 1024, 4096], P('section', ('shard', 'replica'))
- weight_grad: float32 [4, 4096, 512], P('section', 'shard')
All inputs are finite; a program needn't handle non-finite values.
Results may differ from a plain program's by a relative error of at most 0.0058.
Values may be sent and summed in bfloat16 or wider, within the bound.
A program may use at most 64 MiB of HBM per device.

v0:
```python
import functools

import jax
import jax.numpy as jnp
import numpy as np
from jax import lax
from jax.experimental import pallas as pl
from jax.experimental.pallas import tpu as pltpu
from jax.sharding import PartitionSpec as P

HEAD = 128
THETA = 500000.0
EPS = 1e-05
ROWS = 128
PARTS = 2
PIECES = 8
SKEW = 3
F32 = jnp.float32
BF16 = jnp.bfloat16
MESH = pl.DeviceIdType.MESH


def kernel(
    X, S, R,
    acts, grads, saved, kcot, w, gain, pos_f, pos_b, rate,
    keys_o, grad_o, wg_o,
    saved_v, kcot_v, w_v, stream_v, arrived_v,
    sv_recv, kg_all, st_recv, g_buf, g_send, p_buf, p_send, p_own,
    part, from_l, from_r, to_r, to_l, inv_v, tab_v,
    lsem, acts_ss, acts_rs, grads_sem, sv_ss, sv_rs, kg_ss, kg_rs,
    st_ss, st_rs, g_ss, g_rs, p_ss, p_rs, r_ss, r_rs, l_ss, l_rs,
):
    s, j, r = (lax.axis_index(a) for a in ("section", "shard", "replica"))
    T, D = saved.shape
    N = kcot.shape[1]
    Fs = w.shape[0]
    blocks = Fs // ROWS
    C = blocks * PARTS
    width = N // PARTS
    pieces = min(PIECES, blocks)
    Fp = Fs // pieces
    travel = to_r.dtype

    def cols(p, width=Fs, off=0):
        return pl.ds(pl.multiple_of(p * Fs + off, 128), width)

    def peer(d):
        return lax.rem(j + d, S)

    load_saved = pltpu.make_async_copy(saved, saved_v, lsem.at[0])
    load_kcot = pltpu.make_async_copy(kcot, kcot_v, lsem.at[1])
    load_w = pltpu.make_async_copy(w, w_v, lsem.at[2])
    load_acts = pltpu.make_async_copy(acts, stream_v, lsem.at[3])
    load_grads = pltpu.make_async_copy(grads, arrived_v, lsem.at[4])
    load_saved.start()
    load_kcot.start()
    load_w.start()
    pl.when(s == 0)(load_acts.start)
    pl.when(s == X - 1)(load_grads.start)

    barrier = pltpu.get_barrier_semaphore()

    def greet(axis, index):
        pl.semaphore_signal(barrier, inc=1, device_id={axis: index}, device_id_type=MESH)

    for d in range(1, S):
        greet("shard", peer(d))
    pl.when(s > 0)(lambda: greet("section", s - 1))
    pl.when(s < X - 1)(lambda: greet("section", s + 1))
    pl.when(r > 0)(lambda: greet("replica", r - 1))
    pl.when(r < R - 1)(lambda: greet("replica", r + 1))
    peers = S - 1
    for cond in (s > 0, s < X - 1, r > 0, r < R - 1):
        peers = peers + jnp.where(cond, 1, 0)
    pl.semaphore_wait(barrier, peers)

    def remote(src, dst, ss, rs, axis, index):
        return pltpu.make_async_remote_copy(
            src_ref=src, dst_ref=dst, send_sem=ss, recv_sem=rs,
            device_id={axis: index}, device_id_type=MESH,
        )

    def sv_copy(d, q):
        return remote(
            saved.at[:, cols(peer(d), Fp, q * Fp)],
            sv_recv.at[S - d, :, pl.ds(q * Fp, Fp)],
            sv_ss.at[d, q], sv_rs.at[S - d, q], "shard", peer(d),
        )

    def sv_wait(slot, q):
        remote(
            saved.at[:, pl.ds(0, Fp)],
            sv_recv.at[slot, :, pl.ds(pl.multiple_of(q * Fp, 128), Fp)],
            sv_ss.at[slot, q], sv_rs.at[slot, q], "shard", peer(slot),
        ).wait_recv()

    def slot_copy(src, dst, ss, rs, d):
        return remote(src.at[d], dst.at[S - d], ss.at[d], rs.at[S - d], "shard", peer(d))

    def slot_wait(src, dst, ss, rs, slot):
        remote(src.at[slot], dst.at[slot], ss.at[slot], rs.at[slot], "shard", peer(slot)).wait_recv()

    def acts_copy(d):
        return remote(
            acts.at[:, cols(peer(d))], stream_v.at[:, cols(peer(d))],
            acts_ss.at[d], acts_rs.at[d], "section", jnp.minimum(s + 1, X - 1),
        )

    grads_copy = remote(
        grads, arrived_v, grads_sem.at[0], grads_sem.at[1], "section", jnp.maximum(s - 1, 0)
    )

    def kg_copy(d):
        return remote(
            kg_all.at[0], kg_all.at[S - d], kg_ss.at[d], kg_rs.at[S - d], "shard", peer(d)
        )

    def st_copy(d):
        return remote(
            stream_v.at[:, cols(peer(d))], st_recv.at[S - d],
            st_ss.at[d], st_rs.at[S - d], "shard", peer(d),
        )

    def right_copy(c):
        return remote(
            to_r.at[c], from_l.at[c], r_ss.at[c], r_rs.at[c], "replica", jnp.minimum(r + 1, R - 1)
        )

    def left_copy(c):
        return remote(
            to_l.at[c], from_r.at[c], l_ss.at[c], l_rs.at[c], "replica", jnp.maximum(r - 1, 0)
        )

    for d in range(1, S):
        sv_copy(d, 0).start()

    @pl.when(s < X - 1)
    def _():
        for d in (*range(1, S), 0):
            acts_copy(d).start()

    @pl.when(s > 0)
    def _():
        grads_copy.start()

    lane = lax.broadcasted_iota(jnp.int32, (T, HEAD), 1)

    def tables(pos):
        angle = jnp.broadcast_to(pos[...].astype(F32), (T, T)).T[:, :1] * rate[...]
        sine = jnp.sin(angle)
        return jnp.cos(angle), jnp.where(lane < HEAD // 2, -sine, sine)

    def inverse_rms(ref):
        total = jnp.zeros((T, 128), F32)
        for c in range(D // 128):
            v = ref[:, c * 128 : (c + 1) * 128].astype(F32)
            total = total + v * v
        return lax.rsqrt(jnp.sum(total, -1, keepdims=True) / D + EPS)

    cos_b, sin_b = tables(pos_b)
    load_saved.wait()
    load_kcot.wait()
    inverse = inverse_rms(saved_v)
    inv_v[...] = jnp.broadcast_to(inverse, inv_v.shape)
    for h in range(N // HEAD):
        head = slice(h * HEAD, (h + 1) * HEAD)
        v = kcot_v[:, head].astype(F32)
        v = v * cos_b - pltpu.roll(v, HEAD // 2, 1) * sin_b
        kg_all[0, :, head] = (v * inverse).astype(BF16)
    for d in range(1, S):
        kg_copy(d).start()
    for q in range(1, pieces):
        for d in range(1, S):
            sv_copy(d, q).start()

    cos_f, sin_f = tables(pos_f)
    tab_v[0] = cos_f
    tab_v[1] = sin_f
    for d in range(1, S):
        slot_wait(kg_all, kg_all, kg_ss, kg_rs, d)

    def relay():
        pl.when(s == 0)(load_acts.wait)
        for d in range(1, S):
            pl.when(s > 0)(acts_copy(d).wait_recv)
            st_copy(d).start()

    tile = min(512, Fs)

    def backward():
        load_w.wait()

        @pl.loop(0, Fs // tile)
        def _(i):
            at = pl.ds(pl.multiple_of(i * tile, 128), tile)
            m = lax.dot_general(
                kg_all[...].reshape(S * T, N), w_v[at, :], (((1,), (1,)), ((), ())),
                preferred_element_type=F32,
            )
            m = (m * gain[:, cols(j, tile, i * tile)]).astype(BF16)
            g_buf[0, :, at] = m[:T]
            for d in range(1, S):
                g_send[d, :, at] = m[d * T : (d + 1) * T]

        for d in range(1, S):
            slot_copy(g_send, g_buf, g_ss, g_rs, d).start()

    def project(block):
        total = jnp.zeros((T, N), F32)
        for i in range(Fs // tile):
            g = gain[:, cols(j, tile, i * tile)]
            x = (block(i * tile).astype(F32) * g).astype(BF16)
            total = total + jnp.dot(
                x, w_v[i * tile : (i + 1) * tile, :], preferred_element_type=F32
            )
        return total

    def forward_own():
        pl.when(s > 0)(acts_copy(0).wait_recv)
        p_own[...] = project(lambda o: stream_v[:, cols(j, tile, o)])

    def forward_peers():
        for d in range(1, S):
            remote(
                stream_v.at[:, pl.ds(0, Fs)], st_recv.at[d], st_ss.at[d], st_rs.at[d],
                "shard", peer(d),
            ).wait_recv()
            p_send[d] = project(lambda o: st_recv[d, :, o : o + tile]).astype(p_send.dtype)
            slot_copy(p_send, p_buf, p_ss, p_rs, d).start()

    def finish_grad():
        pl.when(s == X - 1)(load_grads.wait)
        pl.when(s < X - 1)(grads_copy.wait_recv)
        for d in range(1, S):
            slot_wait(g_send, g_buf, g_ss, g_rs, d)
        total = jnp.zeros((T, 128), F32)
        for d in range(S):
            for o in range(0, Fs, 128):
                v = saved_v[:, cols(peer(d), 128, o)].astype(F32)
                total = total + v * g_buf[d, :, o : o + 128].astype(F32)
        inv = inv_v[:, :1]
        factor = inv * inv * (jnp.sum(total, -1, keepdims=True) / D)
        for d in range(S):
            for o in range(0, Fs, 128):
                at = cols(peer(d), 128, o)
                v = saved_v[:, at].astype(F32) * factor
                g = arrived_v[:, at].astype(F32) + g_buf[d, :, o : o + 128].astype(F32)
                grad_o[:, at] = (g - v).astype(BF16)

    def finish_keys():
        inv = inverse_rms(stream_v)
        for d in range(1, S):
            slot_wait(p_send, p_buf, p_ss, p_rs, d)
        for h in range(N // HEAD):
            head = slice(h * HEAD, (h + 1) * HEAD)
            v = p_own[:, head]
            for d in range(1, S):
                v = v + p_buf[d, :, head].astype(F32)
            v = v * inv
            v = v * tab_v[0] + pltpu.roll(v, HEAD // 2, 1) * tab_v[1]
            keys_o[:, head] = v.astype(BF16)

    scale = float(T * S * R) ** -0.5

    def when_chunk(c, *conds):
        cond = (c >= 0) & (c < C)
        for extra in conds:
            cond = cond & extra
        return pl.when(cond)

    far = SKEW * jnp.maximum(r, R - 1 - r)
    per_piece = C // pieces
    tasks = {2: relay, 4: backward, 8: forward_own, 14: forward_peers}
    steps = C + SKEW * (R - 1)

    def step(t, carry):
        @pl.when((t < C) & (lax.rem(t, per_piece) == 0))
        def _():
            for d in range(1, S):
                sv_wait(d, t // per_piece)

        @pl.when((t < C) & (lax.rem(t, PARTS) == 0))
        def _():
            o = (t // PARTS) * ROWS
            g = gain[:, cols(j, ROWS, o)]
            sides = [saved_v[:, cols(j, ROWS, o)]]
            for d in range(1, S):
                sides.append(sv_recv[d, :, pl.ds(pl.multiple_of(o, 128), ROWS)])
            x = jnp.concatenate([(v.astype(F32) * g).astype(BF16) for v in sides], 0)
            term = lax.dot_general(
                x, kg_all[...].reshape(S * T, N), (((0,), (0,)), ((), ())),
                preferred_element_type=F32,
            )
            for h in range(PARTS):
                part[t + h] = term[:, h * width : (h + 1) * width]

        a = t - SKEW * r

        @when_chunk(a, r == 0, r < R - 1)
        def _():
            to_r[a] = part[a].astype(travel)
            right_copy(a).start()

        @when_chunk(a, r > 0)
        def _():
            right_copy(a).wait_recv()

        @when_chunk(a, r > 0, r < R - 1)
        def _():
            to_r[a] = (part[a] + from_l[a].astype(F32)).astype(travel)
            right_copy(a).start()

        b = t - SKEW * (R - 1 - r)

        @when_chunk(b, r == R - 1, r > 0)
        def _():
            to_l[b] = part[b].astype(travel)
            left_copy(b).start()

        @when_chunk(b, r < R - 1)
        def _():
            left_copy(b).wait_recv()

        @when_chunk(b, r < R - 1, r > 0)
        def _():
            to_l[b] = (part[b] + from_r[b].astype(F32)).astype(travel)
            left_copy(b).start()

        f = t - far

        def finish(*sums):
            rows = pl.ds(pl.multiple_of((f // PARTS) * ROWS, ROWS), ROWS)
            at = pl.ds(pl.multiple_of(lax.rem(f, PARTS) * width, 128), width)
            total = part[f]
            for ref in sums:
                total = total + ref[f].astype(F32)
            wg_o[rows, at] = total * scale

        when_chunk(f, r == 0, r < R - 1)(lambda: finish(from_r))
        when_chunk(f, r > 0, r < R - 1)(lambda: finish(from_l, from_r))
        when_chunk(f, r > 0, r == R - 1)(lambda: finish(from_l))
        if R == 1:
            when_chunk(f)(finish)

        for at, task in tasks.items():
            pl.when(t == min(at, C - 1))(task)
        pl.when(t == min(26, steps - 1))(finish_grad)
        pl.when(t == min(30, steps - 1))(finish_keys)
        return carry

    lax.fori_loop(0, steps, step, 0)

    for d in range(1, S):
        for q in range(pieces):
            sv_copy(d, q).wait_send()
        kg_copy(d).wait_send()
        st_copy(d).wait_send()
        slot_copy(g_send, g_buf, g_ss, g_rs, d).wait_send()
        slot_copy(p_send, p_buf, p_ss, p_rs, d).wait_send()

    @pl.when(s < X - 1)
    def _():
        for d in range(S):
            acts_copy(d).wait_send()

    @pl.when(s > 0)
    def _():
        grads_copy.wait_send()

    @pl.loop(0, C)
    def _(c):
        pl.when(r < R - 1)(right_copy(c).wait_send)
        pl.when(r > 0)(left_copy(c).wait_send)


def store_kernel(a, b, c, a_out, b_out, c_out, sem):
    copies = [
        pltpu.make_async_copy(src, dst, sem.at[i])
        for i, (src, dst) in enumerate(((c, c_out), (b, b_out), (a, a_out)))
    ]
    for copy in copies:
        copy.start()
    for copy in copies:
        copy.wait()


def per_device(acts_fwd, pos_fwd, saved_acts, pos_bwd, grads_in, key_cotan, weight, gain):
    X, S, R = (lax.axis_size(a) for a in ("section", "shard", "replica"))
    T, D = acts_fwd.shape[1:]
    Fs, N = weight.shape[1:]
    C = Fs // ROWS * PARTS
    width = N // PARTS
    pieces = min(PIECES, Fs // ROWS)
    travel = BF16 if R <= 8 else F32
    index = np.arange(HEAD) % (HEAD // 2)
    rate = jnp.asarray(THETA ** (-(2.0 * index) / HEAD), F32)[None]
    hbm = pl.BlockSpec(memory_space=pltpu.HBM)
    vmem = pl.BlockSpec(memory_space=pltpu.VMEM)
    dma = pltpu.SemaphoreType.DMA
    results = pl.pallas_call(
        functools.partial(kernel, X, S, R),
        out_shape=(
            pltpu.VMEM((T, N), BF16),
            pltpu.VMEM((T, D), BF16),
            pltpu.VMEM((Fs, N), F32),
        ),
        in_specs=[hbm] * 5 + [vmem] * 4,
        out_specs=(vmem, vmem, vmem),
        scratch_shapes=[
            pltpu.VMEM((T, D), BF16),
            pltpu.VMEM((T, N), BF16),
            pltpu.VMEM((Fs, N), BF16),
            pltpu.VMEM((T, D), BF16),
            pltpu.VMEM((T, D), BF16),
            pltpu.VMEM((S, T, Fs), BF16),
            pltpu.VMEM((S, T, N), BF16),
            pltpu.VMEM((S, T, Fs), BF16),
            pltpu.VMEM((S, T, Fs), BF16),
            pltpu.VMEM((S, T, Fs), BF16),
            pltpu.VMEM((S, T, N), BF16),
            pltpu.VMEM((S, T, N), BF16),
            pltpu.VMEM((T, N), F32),
            pltpu.VMEM((C, ROWS, width), F32),
            pltpu.VMEM((C, ROWS, width), travel),
            pltpu.VMEM((C, ROWS, width), travel),
            pltpu.VMEM((C, ROWS, width), travel),
            pltpu.VMEM((C, ROWS, width), travel),
            pltpu.VMEM((T, HEAD), F32),
            pltpu.VMEM((2, T, HEAD), F32),
            dma((5,)),
            dma((S,)), dma((S,)), dma((2,)),
            dma((S, pieces)), dma((S, pieces)),
            dma((S,)), dma((S,)),
            dma((S,)), dma((S,)),
            dma((S,)), dma((S,)),
            dma((S,)), dma((S,)),
            dma((C,)), dma((C,)), dma((C,)), dma((C,)),
        ],
        compiler_params=pltpu.CompilerParams(
            collective_id=0, has_side_effects=True, vmem_limit_bytes=int(57.8 * 2**20)
        ),
        name="relay_window",
    )(
        acts_fwd[0], grads_in[0], saved_acts[0], key_cotan[0], weight[0],
        gain, pos_fwd, pos_bwd, rate,
    )
    keys, grad_out, weight_grad = pl.pallas_call(
        store_kernel,
        out_shape=tuple(jax.ShapeDtypeStruct(v.shape, v.dtype) for v in results),
        in_specs=[vmem] * 3,
        out_specs=[hbm] * 3,
        scratch_shapes=[dma((3,))],
        compiler_params=pltpu.CompilerParams(vmem_limit_bytes=8 * 2**20),
        name="store_results",
    )(*results)
    return keys[None], grad_out[None], weight_grad[None]


def solution(mesh):
    placed = (
        P("section", ("shard", "replica"), None),
        P("section", ("shard", "replica")),
        P("section", ("shard", "replica"), None),
        P("section", ("shard", "replica")),
        P("section", ("shard", "replica"), None),
        P("section", ("shard", "replica"), None),
        P("section", "shard", None),
        P("section", None),
    )
    return jax.shard_map(
        per_device,
        mesh=mesh,
        in_specs=placed,
        out_specs=(
            P("section", ("shard", "replica"), None),
            P("section", ("shard", "replica"), None),
            P("section", "shard", None),
        ),
        check_vma=False,
    )
```

profile of v0, /device:TPU:0, one launch (start us, length us, event | category | flops | bytes accessed | tf_op | source)
XLA Modules:
  0.0 72.3 jit_solution(16884447667577061664)
XLA Ops:
  0.6 69.3 %relay_window.1 = (bf16[128,512]{1,0:T(8,128)(2,1)S(1)}, bf16[128,4096]{1,0:T(8,128)(2,1)S(1)}, f32[2048,512]{1,0:T(8,128)S(1)}) custom-call(bf16[128,4096]{1,0:T(8,128)(2,1)} %bitcast.9, bf16[128,4096]{1,0:T(8,128)(2,1)} %bitcast.10, bf16[128,4096]{1,0:T(8,128)(2,1)} %bitcast.11, bf16[128,512]{1,0:T(8,128)(2,1)} %bitcast.12, bf16[2048,512]{1,0:T(8,128)(2,1)} %bitcast.8, ...), custom_call_target="tpu_custom_call" | custom-call | tf_op jit(solution)/shard_map/relay_window/pallas_call | solution.py:400
  69.9 2.4 %store_results.1 = (bf16[128,512]{1,0:T(8,128)(2,1)}, bf16[128,4096]{1,0:T(8,128)(2,1)}, f32[2048,512]{1,0:T(8,128)}) custom-call(bf16[128,512]{1,0:T(8,128)(2,1)S(1)} %get-tuple-element.9.a, bf16[128,4096]{1,0:T(8,128)(2,1)S(1)} %get-tuple-element.10.b, f32[2048,512]{1,0:T(8,128)S(1)} %get-tuple-element.11.c), custom_call_target="tpu_custom_call" | custom-call | tf_op jit(solution)/shard_map/store_results/pallas_call | solution.py:447
where the time goes:
time: 72.4 us; the launch traced here: 72.3 us
  Pallas kernels  71.6 us (99%)
    pallas_call x1, Pallas kernels, per_device(): pl.pallas_call(functools.partial(kernel, X, S, R), out_shape=(pltpu.VMEM(...  69.3 us
    pallas_call x1, Pallas kernels, per_device(): pl.pallas_call(store_kernel, out_shape=tuple((jax.ShapeDtypeStruct(v.shap...  2.38 us

commit v1 on v0

v1 whole, which is shorter than its diff:
```python
import functools

import jax
import jax.numpy as jnp
import numpy as np
from jax import lax
from jax.experimental import pallas as pl
from jax.experimental.pallas import tpu as pltpu
from jax.sharding import PartitionSpec as P

HEAD = 128
THETA = 500000.0
EPS = 1e-05
ROWS = 128
PARTS = 4
RIGHT = 6
LEFT = 4
LOADS = 2
SENDS = 8
CUTS = 4
SPAN = 64
PLAN = dict(relay=6, backward=8, own=14, peers=36, means=50, grads=54, keys=60)
F32 = jnp.float32
BF16 = jnp.bfloat16
MESH = pl.DeviceIdType.MESH


def sine_cosine(angle):
    turn = jnp.floor(angle * (2.0 / np.pi) + 0.5)
    x = angle - turn * 1.5703125
    x = x - turn * 4.837512969970703125e-4
    x = x - turn * 7.54978995489188216e-8
    y = x * x
    s = ((-1.9515295891e-4 * y + 8.3321608736e-3) * y - 1.6666654611e-1) * y * x + x
    c = (2.443315711809948e-5 * y - 1.388731625493765e-3) * y + 4.166664568298827e-2
    c = c * y * y - 0.5 * y + 1.0
    quarter = turn.astype(jnp.int32) & 3
    odd = (quarter & 1) == 1
    sine, cosine = jnp.where(odd, c, s), jnp.where(odd, s, c)
    sine = jnp.where(quarter >= 2, -sine, sine)
    cosine = jnp.where((quarter == 1) | (quarter == 2), -cosine, cosine)
    return sine, cosine


def pieces_of(blocks):
    pieces, at = [], 0
    while at < blocks:
        size = min(max(at, 1), blocks - at)
        pieces.append((at, size))
        at += size
    return pieces


def rings(C, R):
    ring = min(C, max(RIGHT, LEFT) * (R - 1) + 2)
    return min(C, SENDS), ring, ring


def kernel(
    X, S, R,
    acts, grads, saved, kcot, w, gain_h, pos_f, pos_b, rate_h,
    keys_o, grad_o, wg_o,
    saved_v, kcot_v, w_v, stream_v, arrived_v, gain, posf_v, posb_v, rate,
    sv_recv, kg_all, st_recv, g_buf, g_send, p_buf, p_send, p_acc,
    part, from_l, from_r, to_r, to_l, inv_all, inv_row, tab_v, sum_v, first,
    lsem, saved_sem, acts_ss, acts_rs, grads_sem, sv_ss, sv_rs, kg_ss, kg_rs, iv_ss, iv_rs,
    st_ss, st_rs, g_ss, g_rs, p_ss, p_rs, r_ss, r_rs, l_ss, l_rs,
):
    s, j, r = (lax.axis_index(a) for a in ("section", "shard", "replica"))
    T, D = saved.shape
    N = kcot.shape[1]
    Fs = w.shape[0]
    blocks = Fs // ROWS
    C = blocks * PARTS
    width = N // PARTS
    tile = min(512, Fs)
    tiles = Fs // tile
    wide = min(1024, Fs)
    spans = D // wide
    travel = to_r.dtype
    pieces = pieces_of(blocks)
    sends, right_ring, left_ring = rings(C, R)
    cut = ROWS // CUTS

    barrier = pltpu.get_barrier_semaphore()

    def greet(axis, index):
        pl.semaphore_signal(barrier, inc=1, device_id={axis: index}, device_id_type=MESH)

    def cols(p, width=Fs, off=0):
        return pl.ds(pl.multiple_of(p * Fs + off, 128), width)

    def peer(d):
        return lax.rem(j + d, S)

    for d in range(1, S):
        greet("shard", peer(d))
    pl.when(r > 0)(lambda: greet("replica", r - 1))
    pl.when(r < R - 1)(lambda: greet("replica", r + 1))
    pl.when(s > 0)(lambda: greet("section", s - 1))
    pl.when(s < X - 1)(lambda: greet("section", s + 1))

    load_kcot = pltpu.make_async_copy(kcot, kcot_v, lsem.at[0])
    load_w = pltpu.make_async_copy(w, w_v, lsem.at[0])
    load_acts = pltpu.make_async_copy(acts, stream_v, lsem.at[1])
    load_grads = pltpu.make_async_copy(grads, arrived_v, lsem.at[2])
    load_posb = pltpu.make_async_copy(pos_b, posb_v, lsem.at[1])
    load_posf = pltpu.make_async_copy(pos_f, posf_v, lsem.at[3])
    load_rate = pltpu.make_async_copy(rate_h, rate, lsem.at[2])
    load_gain = pltpu.make_async_copy(gain_h, gain, lsem.at[4])
    Dl = D // LOADS
    load_saved = [
        pltpu.make_async_copy(
            saved.at[:, pl.ds(i * Dl, Dl)], saved_v.at[:, pl.ds(i * Dl, Dl)], saved_sem.at[i]
        )
        for i in range(LOADS)
    ]
    load_posb.start()
    load_rate.start()
    load_kcot.start()
    for copy in load_saved:
        copy.start()
    load_gain.start()
    load_posf.start()

    def remote(src, dst, ss, rs, axis, index):
        return pltpu.make_async_remote_copy(
            src_ref=src, dst_ref=dst, send_sem=ss, recv_sem=rs,
            device_id={axis: index}, device_id_type=MESH,
        )

    def shard_copy(src, dst, ss, rs, d, *index):
        return remote(
            src, dst, ss.at[(d - 1, *index)], rs.at[(S - d - 1, *index)], "shard", peer(d)
        )

    def shard_wait(src, dst, ss, rs, slot, *index):
        remote(
            src, dst, ss.at[(slot - 1, *index)], rs.at[(slot - 1, *index)], "shard", peer(slot)
        ).wait_recv()

    def sv_copy(d, q):
        at, size = (v * ROWS for v in pieces[q])
        return shard_copy(
            saved_v.at[:, cols(peer(d), size, at)], sv_recv.at[S - d, :, pl.ds(at, size)],
            sv_ss, sv_rs, d, q,
        )

    def sv_wait(slot, q):
        at, size = (v * ROWS for v in pieces[q])
        shard_wait(
            saved_v.at[:, pl.ds(0, size)], sv_recv.at[slot, :, pl.ds(at, size)],
            sv_ss, sv_rs, slot, q,
        )

    def kg_copy(d, h):
        at = pl.ds(h * width, width)
        return shard_copy(kg_all.at[0, :, at], kg_all.at[S - d, :, at], kg_ss, kg_rs, d, h)

    def kg_wait(slot, h):
        at = pl.ds(h * width, width)
        shard_wait(kg_all.at[0, :, at], kg_all.at[slot, :, at], kg_ss, kg_rs, slot, h)

    def iv_copy(d):
        return shard_copy(inv_row.at[0], inv_row.at[S - d], iv_ss, iv_rs, d)

    def iv_wait(slot):
        shard_wait(inv_row.at[0], inv_row.at[slot], iv_ss, iv_rs, slot)

    def p_copy(d):
        return shard_copy(p_send.at[d], p_buf.at[S - d], p_ss, p_rs, d)

    def p_wait(slot):
        shard_wait(p_send.at[slot], p_buf.at[slot], p_ss, p_rs, slot)

    def g_copy(d, i):
        at = pl.ds(pl.multiple_of(i * tile, 128), tile)
        return shard_copy(g_send.at[d, :, at], g_buf.at[S - d, :, at], g_ss, g_rs, d, i)

    def g_wait(slot, i):
        at = pl.ds(pl.multiple_of(i * tile, 128), tile)
        shard_wait(g_send.at[slot, :, at], g_buf.at[slot, :, at], g_ss, g_rs, slot, i)

    def acts_copy(d):
        return remote(
            acts.at[:, cols(peer(d))], stream_v.at[:, cols(peer(d))],
            acts_ss.at[d], acts_rs.at[d], "section", jnp.minimum(s + 1, X - 1),
        )

    grads_copy = remote(
        grads, arrived_v, grads_sem.at[0], grads_sem.at[1], "section", jnp.maximum(s - 1, 0)
    )

    def st_copy(d):
        return shard_copy(stream_v.at[:, cols(peer(d))], st_recv.at[S - d], st_ss, st_rs, d)

    def st_wait(slot):
        shard_wait(stream_v.at[:, pl.ds(0, Fs)], st_recv.at[slot], st_ss, st_rs, slot)

    def right_copy(c):
        return remote(
            to_r.at[c], from_l.at[c], r_ss.at[lax.rem(c, sends)], r_rs.at[lax.rem(c, right_ring)],
            "replica", jnp.minimum(r + 1, R - 1),
        )

    def left_copy(c):
        return remote(
            to_l.at[c], from_r.at[c], l_ss.at[lax.rem(c, sends)], l_rs.at[lax.rem(c, left_ring)],
            "replica", jnp.maximum(r - 1, 0),
        )

    def left_cut(i):
        at = pl.ds(i * cut, cut)
        return remote(
            to_l.at[0, at], from_r.at[0, at], l_ss.at[sends + i], l_rs.at[left_ring + i],
            "replica", jnp.maximum(r - 1, 0),
        )

    def send_right(c):
        pl.when(c >= sends)(lambda: right_copy(c - sends).wait_send())
        right_copy(c).start()

    def send_left(c):
        pl.when(c > sends)(lambda: left_copy(c - sends).wait_send())
        left_copy(c).start()

    lane = lax.broadcasted_iota(jnp.int32, (T, HEAD), 1)

    def tables(pos):
        angle = jnp.broadcast_to(pos[...].astype(F32), (T, T)).T[:, :1] * rate[...]
        sine, cosine = sine_cosine(angle)
        return cosine, jnp.where(lane < HEAD // 2, -sine, sine)

    def squares(ref, total, lo, hi):
        for c in range(lo // 128, hi // 128):
            v = ref[:, c * 128 : (c + 1) * 128].astype(F32)
            total = total + v * v
        return total

    def inverse_of(total):
        return lax.rsqrt(jnp.sum(total, -1, keepdims=True) / D + EPS)

    load_posb.wait()
    load_rate.wait()
    cos_b, sin_b = tables(posb_v)
    load_kcot.wait()

    def rotate_back(h):
        for i in range(h * width, (h + 1) * width, HEAD):
            head = slice(i, i + HEAD)
            v = kcot_v[:, head].astype(F32)
            kg_all[0, :, head] = (v * cos_b - pltpu.roll(v, HEAD // 2, 1) * sin_b).astype(BF16)

    rotate_back(0)
    peers = S - 1
    for cond in (s > 0, s < X - 1, r > 0, r < R - 1):
        peers = peers + jnp.where(cond, 1, 0)
    pl.semaphore_wait(barrier, peers)

    def open_exchange():
        for d in range(1, S):
            kg_copy(d, 0).start()
            sv_copy(d, 0).start()

    load_saved[0].wait()
    total = squares(saved_v, jnp.zeros((T, 128), F32), 0, Dl)
    for i in range(1, LOADS):
        load_saved[i].wait()
    pl.when(lax.rem(s, 2) == 0)(open_exchange)
    total = squares(saved_v, total, Dl, D)
    inverse = jnp.broadcast_to(inverse_of(total), (T, 128))
    inv_all[0] = inverse
    inv_row[0] = inverse.T[:8]
    pl.when(lax.rem(s, 2) == 1)(open_exchange)
    for d in range(1, S):
        iv_copy(d).start()
    for h in range(1, PARTS):
        rotate_back(h)
        for d in range(1, S):
            kg_copy(d, h).start()
    for q in range(1, len(pieces)):
        for d in range(1, S):
            sv_copy(d, q).start()
    load_w.start()

    @pl.when(s < X - 1)
    def _():
        for d in (*range(1, S), 0):
            acts_copy(d).start()

    @pl.when(s > 0)
    def _():
        grads_copy.start()

    pl.when(s == 0)(load_acts.start)
    pl.when(s == X - 1)(load_grads.start)
    load_gain.wait()
    load_posf.wait()
    p_acc[...] = jnp.zeros(p_acc.shape, F32)
    sum_v[...] = jnp.zeros(sum_v.shape, F32)

    def rows_of(p):
        o = p * ROWS
        g = gain[:, cols(j, ROWS, o)]
        sides = [saved_v[:, cols(j, ROWS, o)]]
        for d in range(1, S):
            sides.append(sv_recv[d, :, pl.ds(pl.multiple_of(o, 128), ROWS)])
        return jnp.concatenate(
            [(v.astype(F32) * inv_all[d] * g).astype(BF16) for d, v in enumerate(sides)], 0
        )

    def first_term(h):
        at = slice(h * width, (h + 1) * width)
        for d in range(1, S):
            kg_wait(d, h)
        part[h] = lax.dot_general(
            first[...], kg_all[:, :, at].reshape(S * T, width), (((0,), (0,)), ((), ())),
            preferred_element_type=F32,
        )

    def term_of(p):
        for q in range(1, len(pieces)):

            @pl.when(p == pieces[q][0])
            def _():
                for d in range(1, S):
                    sv_wait(d, q)

        term = lax.dot_general(
            rows_of(p), kg_all[...].reshape(S * T, N), (((0,), (0,)), ((), ())),
            preferred_element_type=F32,
        )
        for h in range(PARTS):
            part[p * PARTS + h] = term[:, h * width : (h + 1) * width]

    for d in range(1, S):
        iv_wait(d)
        inv_all[d] = jnp.broadcast_to(inv_row[d][:1], (128, T)).T
        sv_wait(d, 0)
    first[...] = rows_of(0)
    first_term(0)

    def forward_tables():
        cos_f, sin_f = tables(posf_v)
        tab_v[0] = cos_f
        tab_v[1] = sin_f

    def relay():
        pl.when(s == 0)(load_acts.wait)
        for d in range(1, S):
            pl.when(s > 0)(acts_copy(d).wait_recv)
            st_copy(d).start()

    def backward(i):
        pl.when(i == 0)(load_w.wait)
        at = pl.ds(pl.multiple_of(i * tile, 128), tile)
        m = lax.dot_general(
            kg_all[...].reshape(S * T, N), w_v[at, :], (((1,), (1,)), ((), ())),
            preferred_element_type=F32,
        )
        m = (m * gain[:, cols(j, tile, i * tile)]).astype(BF16)
        g_buf[0, :, at] = m[:T]
        for d in range(1, S):
            g_send[d, :, at] = m[d * T : (d + 1) * T]
            g_copy(d, i).start()

    def project(slot, block, i):
        x = (block.astype(F32) * gain[:, cols(j, tile, i * tile)]).astype(BF16)
        at = pl.ds(pl.multiple_of(i * tile, 128), tile)
        p_acc[slot] = p_acc[slot] + jnp.dot(x, w_v[at, :], preferred_element_type=F32)

    def forward_own(i):
        @pl.when((i == 0) & (s > 0))
        def _():
            acts_copy(0).wait_recv()

        project(0, stream_v[:, cols(j, tile, i * tile)], i)

    def forward_peers(i):
        at = pl.ds(pl.multiple_of(i * tile, 128), tile)
        for d in range(1, S):
            @pl.when(i == 0)
            def _():
                st_wait(d)

            project(d, st_recv[d, :, at], i)

            @pl.when(i == tiles - 1)
            def _():
                p_send[d] = p_acc[d].astype(p_send.dtype)
                p_copy(d).start()

    def span_of(q):
        d = q // (Fs // wide)
        return d, lax.rem(q, Fs // wide) * wide

    def grad_means(q):
        @pl.when(q == 0)
        def _():
            for d in range(1, S):
                for i in range(tiles):
                    g_wait(d, i)

        d, o = span_of(q)
        total = sum_v[...]
        for c in range(0, wide, 128):
            v = saved_v[:, cols(peer(d), 128, o + c)].astype(F32)
            total = total + v * g_buf[d, :, pl.ds(pl.multiple_of(o + c, 128), 128)].astype(F32)
        sum_v[...] = total

    def finish_grad(q):
        @pl.when(q == 0)
        def _():
            pl.when(s == X - 1)(load_grads.wait)
            pl.when(s < X - 1)(grads_copy.wait_recv)
            inv = inv_all[0]
            mean = jnp.sum(sum_v[...], -1, keepdims=True) / D
            sum_v[...] = inv * inv * inv * mean

        d, o = span_of(q)
        inv, factor = inv_all[0], sum_v[...]
        for c in range(0, wide, 128):
            at = cols(peer(d), 128, o + c)
            v = saved_v[:, at].astype(F32) * factor
            g = g_buf[d, :, pl.ds(pl.multiple_of(o + c, 128), 128)].astype(F32) * inv
            grad_o[:, at] = (arrived_v[:, at].astype(F32) + g - v).astype(BF16)

    def finish_keys():
        inv = inverse_of(squares(stream_v, jnp.zeros((T, 128), F32), 0, D))
        for d in range(1, S):
            p_wait(d)
        for h in range(N // HEAD):
            head = slice(h * HEAD, (h + 1) * HEAD)
            v = p_acc[0, :, head]
            for d in range(1, S):
                v = v + p_buf[d, :, head].astype(F32)
            v = v * inv
            v = v * tab_v[0] + pltpu.roll(v, HEAD // 2, 1) * tab_v[1]
            keys_o[:, head] = v.astype(BF16)

    scale = float(T * S * R) ** -0.5

    def when_chunk(c, *conds):
        cond = (c >= 0) & (c < C)
        for extra in conds:
            cond = cond & extra
        return pl.when(cond)

    right_lag, left_lag = RIGHT * r, LEFT * (R - 1 - r)
    near, far = jnp.minimum(right_lag, left_lag), jnp.maximum(right_lag, left_lag)
    counts = dict(relay=1, backward=tiles, own=tiles, peers=tiles, means=spans, grads=spans, keys=1)
    start, end = {}, 0
    for name, at in PLAN.items():
        start[name] = max(at * C // SPAN, end)
        end = start[name] + counts[name]
    steps = jnp.maximum(C + far, end)

    def each(t, name, task):
        at = start[name]
        pl.when((t >= at) & (t < at + counts[name]))(lambda: task(t - at))

    def step(t, carry):
        a, b = t - right_lag, t - left_lag

        @pl.when((b == 0) & (r < R - 1))
        def _():
            for i in range(CUTS):
                left_cut(i).wait_recv()
                at = pl.ds(i * cut, cut)

                @pl.when(r > 0)
                def _():
                    to_l[0, at] = (part[0, at] + from_r[0, at].astype(F32)).astype(travel)
                    left_cut(i).start()

        @pl.when((b == 0) & (r == R - 1) & (r > 0))
        def _():
            to_l[0] = part[0].astype(travel)
            for i in range(CUTS):
                left_cut(i).start()

        later = jnp.where(b == 0, -1, b)

        @when_chunk(later, r == R - 1, r > 0)
        def _():
            to_l[b] = part[b].astype(travel)
            send_left(b)

        @when_chunk(a, r == 0, r < R - 1)
        def _():
            to_r[a] = part[a].astype(travel)
            send_right(a)

        @when_chunk(later, r < R - 1)
        def _():
            left_copy(b).wait_recv()

        @when_chunk(later, r < R - 1, r > 0)
        def _():
            to_l[b] = (part[b] + from_r[b].astype(F32)).astype(travel)
            send_left(b)

        @when_chunk(a, r > 0)
        def _():
            right_copy(a).wait_recv()

        @when_chunk(a, r > 0, r < R - 1)
        def _():
            to_r[a] = (part[a] + from_l[a].astype(F32)).astype(travel)
            send_right(a)

        f = t - far

        def finish(*sums):
            rows = pl.ds(pl.multiple_of((f // PARTS) * ROWS, ROWS), ROWS)
            at = pl.ds(pl.multiple_of(lax.rem(f, PARTS) * width, 128), width)
            total = part[f]
            for ref in sums:
                total = total + ref[f].astype(F32)
            wg_o[rows, at] = total * scale

        when_chunk(f, r == 0, r < R - 1)(lambda: finish(from_r))
        when_chunk(f, r > 0, r < R - 1)(lambda: finish(from_l, from_r))
        when_chunk(f, r > 0, r == R - 1)(lambda: finish(from_l))
        if R == 1:
            when_chunk(f)(finish)

        u = t - near
        for h in range(1, PARTS):
            pl.when(u == h - 1)(lambda: first_term(h))
        ahead = u // PARTS + 1

        @pl.when(
            (u >= 0) & (lax.rem(u, PARTS) == jnp.where(u < PARTS, PARTS - 1, 1)) & (ahead < blocks)
        )
        def _():
            term_of(ahead)

        pl.when(t == PARTS)(forward_tables)
        pl.when(t == start["relay"])(relay)
        each(t, "backward", backward)
        each(t, "own", forward_own)
        each(t, "peers", forward_peers)
        each(t, "means", grad_means)
        each(t, "grads", finish_grad)
        pl.when(t == start["keys"])(finish_keys)
        return carry

    lax.fori_loop(0, steps, step, 0)

    for d in range(1, S):
        for q in range(len(pieces)):
            sv_copy(d, q).wait_send()
        for h in range(PARTS):
            kg_copy(d, h).wait_send()
        iv_copy(d).wait_send()
        st_copy(d).wait_send()
        for i in range(tiles):
            g_copy(d, i).wait_send()
        p_copy(d).wait_send()

    @pl.when(s < X - 1)
    def _():
        for d in range(S):
            acts_copy(d).wait_send()

    @pl.when(s > 0)
    def _():
        grads_copy.wait_send()

    @pl.when(r < R - 1)
    def _():
        for c in range(C - sends, C):
            right_copy(c).wait_send()

    @pl.when(r > 0)
    def _():
        for i in range(CUTS):
            left_cut(i).wait_send()
        for c in range(max(C - sends, 1), C):
            left_copy(c).wait_send()


def store_kernel(a, b, c, a_out, b_out, c_out, sem):
    copies = [
        pltpu.make_async_copy(src, dst, sem.at[i])
        for i, (src, dst) in enumerate(((c, c_out), (b, b_out), (a, a_out)))
    ]
    for copy in copies:
        copy.start()
    for copy in copies:
        copy.wait()


def per_device(acts_fwd, pos_fwd, saved_acts, pos_bwd, grads_in, key_cotan, weight, gain):
    X, S, R = (lax.axis_size(a) for a in ("section", "shard", "replica"))
    T, D = acts_fwd.shape[1:]
    Fs, N = weight.shape[1:]
    C = Fs // ROWS * PARTS
    width = N // PARTS
    pieces = len(pieces_of(Fs // ROWS))
    sends, right_ring, left_ring = rings(C, R)
    others = max(S - 1, 1)
    tiles = Fs // min(512, Fs)
    travel = BF16 if R <= 8 else F32
    index = np.arange(HEAD) % (HEAD // 2)
    rate = jnp.asarray(THETA ** (-(2.0 * index) / HEAD), F32)[None]
    hbm = pl.BlockSpec(memory_space=pltpu.HBM)
    vmem = pl.BlockSpec(memory_space=pltpu.VMEM)
    dma = pltpu.SemaphoreType.DMA
    results = pl.pallas_call(
        functools.partial(kernel, X, S, R),
        out_shape=(
            pltpu.VMEM((T, N), BF16),
            pltpu.VMEM((T, D), BF16),
            pltpu.VMEM((Fs, N), F32),
        ),
        in_specs=[hbm] * 9,
        out_specs=(vmem, vmem, vmem),
        scratch_shapes=[
            pltpu.VMEM((T, D), BF16),
            pltpu.VMEM((T, N), BF16),
            pltpu.VMEM((Fs, N), BF16),
            pltpu.VMEM((T, D), BF16),
            pltpu.VMEM((T, D), BF16),
            pltpu.VMEM((1, D), F32),
            pltpu.VMEM((1, T), jnp.int32),
            pltpu.VMEM((1, T), jnp.int32),
            pltpu.VMEM((1, HEAD), F32),
            pltpu.VMEM((S, T, Fs), BF16),
            pltpu.VMEM((S, T, N), BF16),
            pltpu.VMEM((S, T, Fs), BF16),
            pltpu.VMEM((S, T, Fs), BF16),
            pltpu.VMEM((S, T, Fs), BF16),
            pltpu.VMEM((S, T, N), BF16),
            pltpu.VMEM((S, T, N), BF16),
            pltpu.VMEM((S, T, N), F32),
            pltpu.VMEM((C, ROWS, width), F32),
            pltpu.VMEM((C, ROWS, width), travel),
            pltpu.VMEM((C, ROWS, width), travel),
            pltpu.VMEM((C, ROWS, width), travel),
            pltpu.VMEM((C, ROWS, width), travel),
            pltpu.VMEM((S, T, 128), F32),
            pltpu.VMEM((S, 8, T), F32),
            pltpu.VMEM((2, T, HEAD), F32),
            pltpu.VMEM((T, 128), F32),
            pltpu.VMEM((S * T, ROWS), BF16),
            dma((5,)), dma((LOADS,)),
            dma((S,)), dma((S,)), dma((2,)),
            dma((others, pieces)), dma((others, pieces)),
            dma((others, PARTS)), dma((others, PARTS)),
            dma((others,)), dma((others,)),
            dma((others,)), dma((others,)),
            dma((others, tiles)), dma((others, tiles)),
            dma((others,)), dma((others,)),
            dma((sends,)), dma((right_ring,)), dma((sends + CUTS,)), dma((left_ring + CUTS,)),
        ],
        compiler_params=pltpu.CompilerParams(
            collective_id=0, has_side_effects=True, vmem_limit_bytes=int(57.8 * 2**20)
        ),
        name="relay_window",
    )(
        acts_fwd[0], grads_in[0], saved_acts[0], key_cotan[0], weight[0],
        gain, pos_fwd, pos_bwd, rate,
    )
    keys, grad_out, weight_grad = pl.pallas_call(
        store_kernel,
        out_shape=tuple(jax.ShapeDtypeStruct(v.shape, v.dtype) for v in results),
        in_specs=[vmem] * 3,
        out_specs=[hbm] * 3,
        scratch_shapes=[dma((3,))],
        compiler_params=pltpu.CompilerParams(vmem_limit_bytes=8 * 2**20),
        name="store_results",
    )(*results)
    return keys[None], grad_out[None], weight_grad[None]


def solution(mesh):
    placed = (
        P("section", ("shard", "replica"), None),
        P("section", ("shard", "replica")),
        P("section", ("shard", "replica"), None),
        P("section", ("shard", "replica")),
        P("section", ("shard", "replica"), None),
        P("section", ("shard", "replica"), None),
        P("section", "shard", None),
        P("section", None),
    )
    return jax.shard_map(
        per_device,
        mesh=mesh,
        in_specs=placed,
        out_specs=(
            P("section", ("shard", "replica"), None),
            P("section", ("shard", "replica"), None),
            P("section", "shard", None),
        ),
        check_vma=False,
    )
```

time: 72.4 us -> 66.7 us (0.921)
  Pallas kernels: 71.6 us -> 65.9 us
    pallas_call x1, Pallas kernels: 69.3 us -> 63.6 us  [per_device(): pl.pallas_call(functools.partial(kernel, X, S, R), out_shape=(pltpu.VMEM(...]
where the time goes in v1:
time: 66.7 us; the launch traced here: 66.6 us
  Pallas kernels  65.9 us (99%)
    pallas_call x1, Pallas kernels, per_device(): pl.pallas_call(functools.partial(kernel, X, S, R), out_shape=(pltpu.VMEM(...  63.6 us
    pallas_call x1, Pallas kernels, per_device(): pl.pallas_call(store_kernel, out_shape=tuple((jax.ShapeDtypeStruct(v.shap...  2.38 us

profile of v1, /device:TPU:0, one launch (start us, length us, event | category | flops | bytes accessed | tf_op | source)
XLA Modules:
  0.0 66.6 jit_solution(5744885138674068869)
XLA Ops:
  0.6 63.6 %relay_window.1 = (bf16[128,512]{1,0:T(8,128)(2,1)S(1)}, bf16[128,4096]{1,0:T(8,128)(2,1)S(1)}, f32[2048,512]{1,0:T(8,128)S(1)}) custom-call(bf16[128,4096]{1,0:T(8,128)(2,1)} %bitcast.9, bf16[128,4096]{1,0:T(8,128)(2,1)} %bitcast.10, bf16[128,4096]{1,0:T(8,128)(2,1)} %bitcast.11, bf16[128,512]{1,0:T(8,128)(2,1)} %bitcast.12, bf16[2048,512]{1,0:T(8,128)(2,1)} %bitcast.8, ...), custom_call_target="tpu_custom_call" | custom-call | tf_op jit(solution)/shard_map/relay_window/pallas_call | solution.py:611
  64.2 2.4 %store_results.1 = (bf16[128,512]{1,0:T(8,128)(2,1)}, bf16[128,4096]{1,0:T(8,128)(2,1)}, f32[2048,512]{1,0:T(8,128)}) custom-call(bf16[128,512]{1,0:T(8,128)(2,1)S(1)} %get-tuple-element.9.a, bf16[128,4096]{1,0:T(8,128)(2,1)S(1)} %get-tuple-element.10.b, f32[2048,512]{1,0:T(8,128)S(1)} %get-tuple-element.11.c), custom_call_target="tpu_custom_call" | custom-call | tf_op jit(solution)/shard_map/store_results/pallas_call | solution.py:666
